TPU v7x, 128 devices: a whole 4x4x4 slice. The times are simulated.
128 devices in a mesh: shell: 4 (over y_hi, core), img: 32 (over z, y_lo, x).
Axes of the slice: x: 4, y: 4 (y_hi: 2, y_lo: 2; y = y_hi * 2 + y_lo), z: 4, core: 2. Of those that a mesh axis runs over, the one named last changes fastest.
Arguments:
- images: bfloat16 [24576, 16384], P('img', 'shell'), may hold values from -12 to 12, as said below
- references: bfloat16 [1024, 16384], P('img', 'shell'), may hold values from -1 to 1, as said below
- shell_of_pixel: int32 [16384], P('shell'), may hold values from 0 to 63
- noise_power: float32 [64], replicated, may hold values from 0.1 to 10
- ref_class: int32 [1024], replicated, may hold values from 0 to 3
- ref_orient: int32 [1024], replicated, may hold values from 0 to 6143
- class_logw: float32 [4], replicated, may hold values from -4 to 4
- orient_logw: float32 [6144], replicated, may hold values from -4 to 4
Outputs:
- accumulators: float32 [1024, 16384], P('img', 'shell')
- evidence_logarithm: float32 [24576], P('img')
Inputs may be any that keep to these rules, and one draw needn't show every extreme that they name: `images`: images are real-valued Fourier data. `references`: references are real-valued projections.
All inputs are finite; a program needn't handle non-finite values.
Results may differ from a plain program's by a relative error of at most 0.0077.
Values may be sent and summed in bfloat16 or wider, within the bound.
A program may use at most 128 MiB of HBM per device.

v0:
```python
import jax
import jax.numpy as jnp
from jax import lax
from jax.sharding import PartitionSpec as P

inverse_heat_factor = 0.5


def split_up(array, dim, peers):
    dims = array.shape
    tiles = array.reshape(*dims[:dim], peers, dims[dim] // peers, *dims[dim + 1 :])
    return jnp.moveaxis(tiles, dim, 0)


def sum_at_owner(array, axis, dim):
    peers = lax.axis_size(axis)
    tiles = lax.all_to_all(split_up(array, dim, peers), axis, 0, 0, tiled=True)
    return jnp.sum(tiles, axis=0)


def sent_to_all(array, axis):
    peers = lax.axis_size(axis)
    return lax.all_to_all(
        jnp.broadcast_to(array[None], (peers, *array.shape)), axis, 0, 0, tiled=True
    )


def in_order(tiles, dim):
    dims = list(tiles.shape[1:])
    dims[dim] *= tiles.shape[0]
    return jnp.moveaxis(tiles, 0, dim).reshape(dims)


def gathered_copies(array, axis, dim):
    tiles = sent_to_all(array, axis)
    return in_order(tiles, dim)


def tempered_softmax(overall_total, beforehand_logarithmic_share):
    raw_logarithmic_measures = (
        inverse_heat_factor * overall_total + beforehand_logarithmic_share[None, :]
    )
    highest = jnp.max(raw_logarithmic_measures, axis=1)
    evidence_logarithm = highest + jnp.log(
        jnp.sum(jnp.exp(raw_logarithmic_measures - highest[:, None]), axis=1)
    )
    posterior = jnp.exp(raw_logarithmic_measures - evidence_logarithm[:, None]).astype(jnp.bfloat16)
    return (posterior, evidence_logarithm)


def shards(
    images, references, shell_of_pixel, noise_power, ref_class, ref_orient, class_logw, orient_logw
):
    inverse_noise = 1.0 / noise_power
    matches = shell_of_pixel[:, None] == jnp.arange(noise_power.shape[0], dtype=jnp.int32)[None, :]
    weights = jnp.sum(jnp.where(matches, inverse_noise[None, :], jnp.float32(0.0)), axis=1)
    weighted = (images.astype(jnp.float32) * weights[None, :]).astype(jnp.bfloat16)
    reference_block_list = lax.all_gather(references, "img", axis=0, tiled=True)
    correlation = lax.dot_general(
        weighted, reference_block_list, (((1,), (1,)), ((), ())), preferred_element_type=jnp.float32
    )
    block_float = reference_block_list.astype(jnp.float32)
    ref_norm = jnp.dot(block_float * block_float, weights, precision=lax.Precision.HIGHEST)
    incomplete_measures = correlation - 0.5 * ref_norm[None, :]
    class_agreement = (
        ref_class[:, None] == jnp.arange(class_logw.shape[0], dtype=jnp.int32)[None, :]
    )
    beforehand_logarithmic_share = (
        jnp.sum(jnp.where(class_agreement, class_logw[None, :], jnp.float32(0.0)), axis=1)
        + orient_logw[ref_orient]
    )
    score_rows = sum_at_owner(incomplete_measures, "shell", 0)
    row_posterior, row_log_marginal = tempered_softmax(score_rows, beforehand_logarithmic_share)
    posterior, evidence_logarithm = (
        gathered_copies(row_posterior, "shell", 0),
        gathered_copies(row_log_marginal.astype(jnp.bfloat16), "shell", 0).astype(
            row_log_marginal.dtype
        ),
    )
    accumulators = lax.psum_scatter(
        lax.dot_general(
            posterior, images, (((0,), (0,)), ((), ())), preferred_element_type=jnp.float32
        ),
        "img",
        scatter_dimension=0,
        tiled=True,
    )
    return (accumulators, evidence_logarithm)


def solution(mesh):
    placed = (P("img", "shell"), P("img", "shell"), P("shell"), P(), P(), P(), P(), P())
    return jax.shard_map(
        shards, mesh=mesh, in_specs=placed, out_specs=(P("img", "shell"), P("img")), check_vma=False
    )
```

profile of v0, /device:TPU:0, one launch (start us, length us, event | category | flops | bytes accessed | tf_op | source)
XLA Modules:
  0.0 501.9 jit_solution(11843192143524128233)
XLA Ops:
  7.2 0.0 copy-start
  7.2 0.0 all-gather.2.cloned.1.call-start
  7.2 0.7 all-gather.2.cloned.1.call-update
  7.9 0.7 broadcast_divide_fusion
  8.6 1.0 select_reduce_fusion
  9.5 168.8 %all-gather.2.cloned.1.call-done = bf16[1024,4096]{1,0:T(8,128)(2,1)} async-done(((bf16[32,4096]{1,0:T(8,128)(2,1)}), bf16[1024,4096]{1,0:T(8,128)(2,1)}) %all-gather.2.cloned.1.call-update) | async-done | bytes 8388624 | tf_op jit(solution)/shard_map/all_gather | solution.py:58
  178.3 0.0 copy-start.1
  178.3 18.0 %fusion = f32[1,1024]{1,0:T(1,128)S(1)} fusion(f32[4096,1]{0,1:T(1,128)S(1)} %bitcast.10, bf16[1024,4096]{1,0:T(8,128)(2,1)} %all-gather.2.cloned.1.call-done), kind=kOutput, calls=%fused_computation.1 | convolution fusion | flops 58720256 | bytes 8409088 | tf_op jit(solution)/shard_map/dot_general | solution.py:63
  196.3 0.0 copy-done.1
  196.4 10.3 %fusion.5 = f32[768,1024]{1,0:T(8,128)} fusion(bf16[1024,4096]{1,0:T(8,128)(2,1)S(1)} %copy-done.1, bf16[768,4096]{1,0:T(8,128)(2,1)} %param.8, f32[4096]{0:T(1024)S(1)} %select_reduce_fusion, f32[1024]{0:T(1024)S(1)} %broadcast_multiply_fusion), kind=kOutput, calls=%fused_computation.7 | convolution fusion | flops 6452674560 | bytes 17846272 | tf_op jit(solution)/shard_map/dot_general | solution.py:59
  206.6 0.0 copy-start.2
  206.6 0.0 copy-start.3
  206.6 4.3 all-to-all-start
  210.9 0.0 reduce-scatter.2.cloned.1.call-start
  210.9 0.0 copy-done.2
  210.9 0.0 copy-done
  210.9 6.2 %gather_fusion = f32[1024]{0:T(1024)S(1)} fusion(f32[6144]{0:T(1024)S(1)} %copy-done, s32[1024]{0:T(1024)S(1)} %fusion.7), kind=kCustom, calls=%fused_computation | custom fusion | bytes 12288 | tf_op jit(solution)/shard_map/gather | solution.py:70
  217.1 0.0 copy-done.3
  217.1 0.0 copy-done.4
  217.1 0.1 select_reduce_fusion.1
  217.2 32.1 %all-to-all-done = f32[4,192,1024]{2,1,0:T(8,128)S(1)} async-done(((f32[4,192,1024]{2,1,0:T(8,128)}), f32[4,192,1024]{2,1,0:T(8,128)S(1)}, u32[]{:S(2)}, u32[]{:S(2)}) %all-to-all-start) | async-done | bytes 3145760 | tf_op jit(solution)/shard_map/all_to_all | solution.py:17
  249.3 1.2 reduce_sum.37
  250.5 1.3 fusion.6
  251.8 1.4 exponential_reduce_fusion
  253.2 1.3 exponential_convert_fusion
  254.6 0.2 broadcast_in_dim.35
  254.8 24.0 %all_to_all.16 = bf16[4,192,1024]{2,1,0:T(8,128)(2,1)S(1)} all-to-all(bf16[4,192,1024]{2,1,0:T(8,128)(2,1)S(1)} %broadcast_in_dim.35), channel_id=1, replica_groups=mesh['shell'=4,'img'=32] {'shell'}, dimensions={0} | all-to-all | bytes 3145728 | tf_op jit(solution)/shard_map/all_to_all | solution.py:23
  278.8 13.0 %fusion.9 = f32[1024,4096]{1,0:T(8,128)} fusion(bf16[768,1024]{1,0:T(8,128)(2,1)S(1)} %bitcast.8, bf16[768,4096]{1,0:T(8,128)(2,1)} %param.8), kind=kOutput, calls=%fused_computation.23 | convolution fusion | flops 6442450944 | bytes 24641536 | tf_op jit(solution)/shard_map/dot_general | solution.py:81
  291.8 0.0 reduce-scatter.2.cloned.1.call-update
  291.8 7.6 %all_to_all.17 = bf16[4,1,192]{2,1,0:T(2,128)(2,1)S(1)} all-to-all(bf16[4,1,192]{2,1,0:T(2,128)(2,1)S(1)} %broadcast_in_dim.56), channel_id=1, replica_groups=mesh['shell'=4,'img'=32] {'shell'}, dimensions={0} | all-to-all | bytes 3072 | tf_op jit(solution)/shard_map/all_to_all | solution.py:23
  299.5 0.7 reshape.81
  300.2 194.9 %reduce-scatter.2.cloned.1.call-done = f32[32,4096]{1,0:T(8,128)} async-done(((f32[1024,4096]{1,0:T(8,128)}), f32[32,4096]{1,0:T(8,128)}) %reduce-scatter.2.cloned.1.call-update) | async-done | bytes 524304 | tf_op jit(solution)/shard_map/reduce_scatter | solution.py:80
  (7 shorter events, 0.1 us)
Async XLA Ops:
  7.2 203.7 %copy-start = (f32[6144]{0:T(1024)S(1)}, f32[6144]{0:T(1024)}, u32[]{:S(2)}) copy-start(f32[6144]{0:T(1024)} %param.15) | copy-start | bytes 73732
  7.2 171.1 %all-gather.2.cloned.1.call-start = ((), (), s32[]{:S(2)}) async-start(), calls=%async_computation.4 | async-start | bytes 8650752 | tf_op jit(solution)/shard_map/all_gather | solution.py:58
  178.3 18.0 %copy-start.1 = (bf16[1024,4096]{1,0:T(8,128)(2,1)S(1)}, bf16[1024,4096]{1,0:T(8,128)(2,1)}, u32[]{:S(2)}) copy-start(bf16[1024,4096]{1,0:T(8,128)(2,1)} %all-gather.2.cloned.1.call-done) | copy-start | bytes 25165828
  206.6 4.3 copy-start.2
  206.6 10.5 %copy-start.3 = (s32[1024]{0:T(1024)S(1)}, s32[1024]{0:T(1024)}, u32[]{:S(2)}) copy-start(s32[1024]{0:T(1024)} %param.12) | copy-start | bytes 12292
  206.6 10.5 %copy-start.4 = (f32[4]{0:T(128)S(1)}, f32[4]{0:T(128)}, u32[]{:S(2)}) copy-start(f32[4]{0:T(128)} %param.14) | copy-start | bytes 52
  206.6 42.7 %all-to-all-start = ((f32[4,192,1024]{2,1,0:T(8,128)}), f32[4,192,1024]{2,1,0:T(8,128)S(1)}, u32[]{:S(2)}, u32[]{:S(2)}) async-start(f32[4,192,1024]{2,1,0:T(8,128)} %bitcast.9), calls=%async_computation | async-start | bytes 6291456 | tf_op jit(solution)/shard_map/all_to_all | solution.py:17
  210.9 284.2 %reduce-scatter.2.cloned.1.call-start = ((), (), s32[]{:S(2)}) async-start(), calls=%async_computation.5 | async-start | bytes 17301504 | tf_op jit(solution)/shard_map/reduce_scatter | solution.py:80
Sparse Core Ops, SparseCore 0:
  9.6 168.6 all-gather.1
  291.9 203.1 reduce-scatter.1
where the time goes:
time: 502 us
  waiting for transfers between devices  397 us (79%)
  matrix products  41.3 us (8%)
  blocking collectives  31.6 us (6%)
  between operations  14.1 us (3%)
  local copies, waits for them, and re-layouts  7.06 us (1%)
  other arithmetic  6.99 us (1%)
    reduce_scatter x1, waiting for transfers between devices, shards(): lax.psum_scatter(lax.dot_general(posterior, images, (((0,), (0,)), ((), (...  195 us
    all_gather x1, waiting for transfers between devices, shards(): reference_block_list = lax.all_gather(references, 'img', axis=0, tiled=True)  169 us
    all_to_all x1, waiting for transfers between devices, sum_at_owner(): tiles = lax.all_to_all(split_up(array, dim, peers), axis, 0, 0, tiled=True)  32.1 us
    all_to_all x2, blocking collectives, sent_to_all(): lax.all_to_all(jnp.broadcast_to(array[None], (peers, *array.shape)), axis...  31.6 us
    dot_general x1, matrix products, shards(): jnp.dot(block_float * block_float, weights, precision=lax.Precision.HIGHEST)  18 us
    dot_general x1, matrix products, shards(): lax.dot_general(posterior, images, (((0,), (0,)), ((), ())), preferred_el...  13 us
    dot_general x1, matrix products, shards(): lax.dot_general(weighted, reference_block_list, (((1,), (1,)), ((), ())),...  10.3 us
  transfers between devices with their start and end apart: 3, of which 3 were waited for; matrix products, arithmetic and copies ran while one was open for 2% of the time, Pallas kernels for 0%

commit v1 on v0

--- a/solution.py
+++ b/solution.py
@@ -55,7 +55,8 @@
     matches = shell_of_pixel[:, None] == jnp.arange(noise_power.shape[0], dtype=jnp.int32)[None, :]
     weights = jnp.sum(jnp.where(matches, inverse_noise[None, :], jnp.float32(0.0)), axis=1)
     weighted = (images.astype(jnp.float32) * weights[None, :]).astype(jnp.bfloat16)
-    reference_block_list = lax.all_gather(references, "img", axis=0, tiled=True)
+    repeated = jnp.stack([references] * lax.axis_size("img"))
+    reference_block_list = jnp.concatenate(lax.all_to_all(repeated, "img", 0, 0), axis=0)
     correlation = lax.dot_general(
         weighted, reference_block_list, (((1,), (1,)), ((), ())), preferred_element_type=jnp.float32
     )

time: 502 us -> 469 us (0.934)
  waiting for transfers between devices: 397 us -> 348 us
  starting transfers between devices: 4.3 us -> 13.9 us
  local copies, waits for them, and re-layouts: 7.06 us -> 12.3 us
    all_gather x1 -> x0, waiting for transfers between devices: 169 us -> none  [shards(): reference_block_list = lax.all_gather(references, 'img', axis=0, tiled=True)]
    all_to_all x0 -> x1, waiting for transfers between devices: none -> 119 us  [shards(): lax.all_to_all(repeated, 'img', 0, 0)]
    all_to_all x0 -> x1, starting transfers between devices: none -> 9.55 us  [shards(): lax.all_to_all(repeated, 'img', 0, 0)]
    another operation x0 -> x1, local copies, waits for them, and re-layouts: none -> 5.21 us  [shards(): repeated = jnp.stack([references] * lax.axis_size('img'))]
where the time goes in v1:
time: 469 us
  waiting for transfers between devices  348 us (74%)
  matrix products  42.5 us (9%)
  blocking collectives  31.6 us (7%)
  between operations  14.1 us (3%)
  starting transfers between devices  13.9 us (3%)
  local copies, waits for them, and re-layouts  12.3 us (3%)
  other arithmetic  5.62 us (1%)
    reduce_scatter x1, waiting for transfers between devices, shards(): lax.psum_scatter(lax.dot_general(posterior, images, (((0,), (0,)), ((), (...  197 us
    all_to_all x1, waiting for transfers between devices, shards(): lax.all_to_all(repeated, 'img', 0, 0)  119 us
    all_to_all x1, waiting for transfers between devices, sum_at_owner(): tiles = lax.all_to_all(split_up(array, dim, peers), axis, 0, 0, tiled=True)  32.1 us
    all_to_all x2, blocking collectives, sent_to_all(): lax.all_to_all(jnp.broadcast_to(array[None], (peers, *array.shape)), axis...  31.6 us
    dot_general x1, matrix products, shards(): jnp.dot(block_float * block_float, weights, precision=lax.Precision.HIGHEST)  17.3 us
    dot_general x1, matrix products, shards(): lax.dot_general(posterior, images, (((0,), (0,)), ((), ())), preferred_el...  13 us
    dot_general x1, matrix products, shards(): lax.dot_general(weighted, reference_block_list, (((1,), (1,)), ((), ())),...  12.2 us
    all_to_all x1, starting transfers between devices, shards(): lax.all_to_all(repeated, 'img', 0, 0)  9.55 us
  transfers between devices with their start and end apart: 3, of which 3 were waited for; matrix products, arithmetic and copies ran while one was open for 2% of the time, Pallas kernels for 0%

profile of v1, /device:TPU:0, one launch (start us, length us, event | category | flops | bytes accessed | tf_op | source)
XLA Modules:
  0.0 468.5 jit_solution(17333248540586792509)
XLA Ops:
  7.2 0.0 copy-start
  7.2 5.2 %stack.2 = bf16[32,32,4096]{2,1,0:T(8,128)(2,1)} broadcast(bf16[32,4096]{1,0:T(8,128)(2,1)} %param.9), dimensions={1,2} | broadcast | bytes 8650752 | tf_op jit(solution)/shard_map/stack | solution.py:58
  12.4 0.0 copy-start.5
  12.4 0.0 copy-start.1
  12.4 9.5 %all-to-all-start = ((bf16[32,32,4096]{2,1,0:T(8,128)(2,1)}), bf16[32,32,4096]{2,1,0:T(8,128)(2,1)}, u32[]{:S(2)}, u32[]{:S(2)}) async-start(bf16[32,32,4096]{2,1,0:T(8,128)(2,1)} %stack.2), calls=%async_computation | async-start | bytes 16777216 | tf_op jit(solution)/shard_map/all_to_all | solution.py:59
  21.9 0.0 copy-done.5
  22.0 0.0 copy-done.1
  22.0 0.2 select_reduce_fusion
  22.2 119.3 %all-to-all-done = bf16[32,32,4096]{2,1,0:T(8,128)(2,1)} async-done(((bf16[32,32,4096]{2,1,0:T(8,128)(2,1)}), bf16[32,32,4096]{2,1,0:T(8,128)(2,1)}, u32[]{:S(2)}, u32[]{:S(2)}) %all-to-all-start) | async-done | bytes 8388640 | tf_op jit(solution)/shard_map/all_to_all | solution.py:59
  141.5 17.3 %fusion = f32[1,1024]{1,0:T(1,128)S(1)} fusion(f32[4096,1]{0,1:T(1,128)S(1)} %bitcast.11, bf16[1024,4096]{1,0:T(8,128)(2,1)} %bitcast), kind=kOutput, calls=%fused_computation.1 | convolution fusion | flops 58720256 | bytes 8409088 | tf_op jit(solution)/shard_map/dot_general | solution.py:64
  158.7 12.2 %fusion.5 = f32[768,1024]{1,0:T(8,128)} fusion(bf16[1024,4096]{1,0:T(8,128)(2,1)} %bitcast, bf16[768,4096]{1,0:T(8,128)(2,1)} %param.8, f32[4096]{0:T(1024)S(1)} %select_reduce_fusion, f32[1024]{0:T(1024)S(1)} %broadcast_multiply_fusion), kind=kOutput, calls=%fused_computation.7 | convolution fusion | flops 6452674560 | bytes 17846272 | tf_op jit(solution)/shard_map/dot_general | solution.py:60
  171.0 0.0 copy-start.2
  171.0 4.3 all-to-all-start.1
  175.3 0.0 reduce-scatter.2.cloned.1.call-start
  175.3 0.0 copy-done.2
  175.3 0.0 copy-done
  175.3 6.2 %gather_fusion = f32[1024]{0:T(1024)S(1)} fusion(f32[6144]{0:T(1024)S(1)} %copy-done, s32[1024]{0:T(1024)S(1)} %fusion.7), kind=kCustom, calls=%fused_computation | custom fusion | bytes 12288 | tf_op jit(solution)/shard_map/gather | solution.py:71
  181.5 0.0 copy-done.3
  181.5 0.0 copy-done.4
  181.5 0.1 select_reduce_fusion.1
  181.6 32.1 %all-to-all-done.1 = f32[4,192,1024]{2,1,0:T(8,128)S(1)} async-done(((f32[4,192,1024]{2,1,0:T(8,128)}), f32[4,192,1024]{2,1,0:T(8,128)S(1)}, u32[]{:S(2)}, u32[]{:S(2)}) %all-to-all-start.1) | async-done | bytes 3145760 | tf_op jit(solution)/shard_map/all_to_all | solution.py:17
  213.7 1.2 reduce_sum.37
  214.9 1.3 fusion.6
  216.2 1.4 exponential_reduce_fusion
  217.6 1.3 exponential_convert_fusion
  219.0 0.2 broadcast_in_dim.35
  219.2 24.0 %all_to_all.21 = bf16[4,192,1024]{2,1,0:T(8,128)(2,1)S(1)} all-to-all(bf16[4,192,1024]{2,1,0:T(8,128)(2,1)S(1)} %broadcast_in_dim.35), channel_id=1, replica_groups=mesh['shell'=4,'img'=32] {'shell'}, dimensions={0} | all-to-all | bytes 3145728 | tf_op jit(solution)/shard_map/all_to_all | solution.py:23
  243.2 13.0 %fusion.9 = f32[1024,4096]{1,0:T(8,128)} fusion(bf16[768,1024]{1,0:T(8,128)(2,1)S(1)} %bitcast.9, bf16[768,4096]{1,0:T(8,128)(2,1)} %param.8), kind=kOutput, calls=%fused_computation.23 | convolution fusion | flops 6442450944 | bytes 24641536 | tf_op jit(solution)/shard_map/dot_general | solution.py:82
  256.2 0.0 reduce-scatter.2.cloned.1.call-update
  256.2 7.6 %all_to_all.22 = bf16[4,1,192]{2,1,0:T(2,128)(2,1)S(1)} all-to-all(bf16[4,1,192]{2,1,0:T(2,128)(2,1)S(1)} %broadcast_in_dim.56), channel_id=1, replica_groups=mesh['shell'=4,'img'=32] {'shell'}, dimensions={0} | all-to-all | bytes 3072 | tf_op jit(solution)/shard_map/all_to_all | solution.py:23
  263.9 0.7 reshape.87
  264.6 197.1 %reduce-scatter.2.cloned.1.call-done = f32[32,4096]{1,0:T(8,128)} async-done(((f32[1024,4096]{1,0:T(8,128)}), f32[32,4096]{1,0:T(8,128)}) %reduce-scatter.2.cloned.1.call-update) | async-done | bytes 524304 | tf_op jit(solution)/shard_map/reduce_scatter | solution.py:81
  (9 shorter events, 0.1 us)
Async XLA Ops:
  7.2 168.2 %copy-start = (f32[6144]{0:T(1024)S(1)}, f32[6144]{0:T(1024)}, u32[]{:S(2)}) copy-start(f32[6144]{0:T(1024)} %param.15) | copy-start | bytes 73732
  12.4 9.6 %copy-start.5 = (f32[64]{0:T(128)S(1)}, f32[64]{0:T(128)}, u32[]{:S(2)}) copy-start(f32[64]{0:T(128)} %param.11) | copy-start | bytes 772
  12.4 9.6 %copy-start.1 = (s32[4096]{0:T(1024)S(1)}, s32[4096]{0:T(1024)}, u32[]{:S(2)}) copy-start(s32[4096]{0:T(1024)} %param.10) | copy-start | bytes 49156
  12.4 129.1 %all-to-all-start = ((bf16[32,32,4096]{2,1,0:T(8,128)(2,1)}), bf16[32,32,4096]{2,1,0:T(8,128)(2,1)}, u32[]{:S(2)}, u32[]{:S(2)}) async-start(bf16[32,32,4096]{2,1,0:T(8,128)(2,1)} %stack.2), calls=%async_computation | async-start | bytes 16777216 | tf_op jit(solution)/shard_map/all_to_all | solution.py:59
  171.0 4.3 copy-start.2
  171.0 10.5 %copy-start.3 = (s32[1024]{0:T(1024)S(1)}, s32[1024]{0:T(1024)}, u32[]{:S(2)}) copy-start(s32[1024]{0:T(1024)} %param.12) | copy-start | bytes 12292
  171.0 10.5 %copy-start.4 = (f32[4]{0:T(128)S(1)}, f32[4]{0:T(128)}, u32[]{:S(2)}) copy-start(f32[4]{0:T(128)} %param.14) | copy-start | bytes 52
  171.0 42.7 %all-to-all-start.1 = ((f32[4,192,1024]{2,1,0:T(8,128)}), f32[4,192,1024]{2,1,0:T(8,128)S(1)}, u32[]{:S(2)}, u32[]{:S(2)}) async-start(f32[4,192,1024]{2,1,0:T(8,128)} %bitcast.10), calls=%async_computation.1 | async-start | bytes 6291456 | tf_op jit(solution)/shard_map/all_to_all | solution.py:17
  175.3 286.4 %reduce-scatter.2.cloned.1.call-start = ((), (), s32[]{:S(2)}) async-start(), calls=%async_computation.5 | async-start | bytes 17301504 | tf_op jit(solution)/shard_map/reduce_scatter | solution.py:81
Sparse Core Ops, SparseCore 0:
  256.4 205.2 reduce-scatter.1
